TPU v7x, 32 devices: a whole 2x2x4 slice. The times are simulated.
32 devices in a mesh: lon: 8 (over z, x), lat: 4 (over y, core).
Axes of the slice: x: 2, y: 2, z: 4, core: 2. Of those that a mesh axis runs over, the one named last changes fastest.
Arguments:
- tracers: float32 [40, 8, 32, 1024], P(None, None, 'lat', 'lon'), may hold values from -6 to 6
- kmt: int32 [32, 1024], P('lat', 'lon'), may hold values from 0 to 8
Outputs:
- updated: float32 [40, 8, 32, 1024], P(None, None, 'lat', 'lon')
Inputs may be any that keep to these rules, and one draw needn't show every extreme that they name: Level k of column (j, i) is ocean exactly when k < kmt[j, i].
All inputs are finite; a program needn't handle non-finite values.
Results may differ from a plain program's by a relative error of at most 0.00002.
Values sent between devices are 32-bit elements; how exact they have to be, the bound alone decides.
A program may use at most 64 MiB of HBM per device.

v0:
```python
import functools

import jax
import jax.numpy as jnp
from jax import lax
from jax.experimental import pallas as pl
from jax.experimental.pallas import tpu as pltpu
from jax.sharding import PartitionSpec as P

THERMAL = 0.2
HALINE = 0.8
REDI = 0.1
SKEW = 0.05
SLOPE_MAX = 0.6
SLOPE_WIDTH = 0.2

MESH = pl.DeviceIdType.MESH
TOGETHER = 2
QUAD = 4
C, E, W, N, S = range(5)


def taper(slope):
    return slope * 0.5 * (1.0 + jnp.tanh((SLOPE_MAX - jnp.abs(slope)) / SLOPE_WIDTH))


def column(rho, wet, up, dn):
    hi = wet * dn(wet)
    strat = (dn(rho) - rho) * hi
    return rho, wet, hi, up(hi), 0.5 * (strat + up(strat))


def line(c, p, m, up, dn):
    c_rho, c_wet, c_hi, c_lo, c_cell = c
    p_rho, p_wet, p_hi, p_lo, p_cell = p
    m_rho, m_wet, m_hi, m_lo, m_cell = m
    mp, mm = c_wet * p_wet, c_wet * m_wet
    sp = taper((p_rho - c_rho) * mp / jnp.maximum(0.5 * (p_cell + c_cell), 1.0))
    sm = taper((c_rho - m_rho) * mm / jnp.maximum(0.5 * (m_cell + c_cell), 1.0))
    cx = 0.5 * (sp + sm)
    sw = 0.5 * (cx + dn(cx))
    fh = ((REDI + SKEW) * 0.25) * sw * c_hi
    zh = REDI * (sw * sw) * c_hi
    fl, zl = up(fh), up(zh)
    pp = ((REDI - SKEW) * 0.25) * sp * mp
    pm = -((REDI - SKEW) * 0.25) * sm * mm
    own_p, own_m = mp * (fh - fl), mm * (fl - fh)
    mph, mmh = dn(mp) * fh, dn(mm) * fh
    mpl, mml = up(mp) * fl, up(mm) * fl
    q = pp + pm
    return (
        (mpl - mml - q * c_lo + zl,
         q * (c_lo - c_hi) - REDI * (mp + mm) - (own_p + own_m) - (zh + zl),
         mmh - mph + q * c_hi + zh),
        (-pp * p_lo - mpl, REDI * mp + pp * (p_lo - p_hi) + own_p, pp * p_hi + mph),
        (mml - pm * m_lo, REDI * mm + pm * (m_lo - m_hi) + own_m, pm * m_hi - mmh),
    )


def total(terms):
    result = terms[0]
    for term in terms[1:]:
        result = result + term
    return result


def kernel(
    sizes, x_ref, kmt_ref, out_ref,
    xv, kmt_int, coef, wcol, ecol, inner_w, inner_e, west, east, from_n, from_s, kmt_n, kmt_s,
    load_sem, send_sem, recv_sem,
):
    tracers, levels, rows, lanes, n_lon, n_lat = sizes
    lon, lat = lax.axis_index("lon"), lax.axis_index("lat")
    at_top = lat == n_lat - 1
    below_top = jnp.logical_not(at_top)
    inner = lat > 0
    at_bottom = jnp.logical_not(inner)
    e_dev = (lax.rem(lon + 1, n_lon), lat)
    w_dev = (lax.rem(lon + n_lon - 1, n_lon), lat)
    n_dev, s_dev = (lon, lat + 1), (lon, lat - 1)
    fold_dev = (n_lon - 1 - lon, lat)
    tiles = tracers * levels
    plane = levels * rows
    quad = lanes // QUAD
    head = tiles % lanes
    regs = tiles // lanes + 1
    quads = tiles // quad
    per_piece = head // quad
    piece = head
    pieces = tiles // piece
    bounds = [0] + [head + lanes * j for j in range(regs)]

    barrier = pltpu.get_barrier_semaphore()

    def greet(dev):
        pl.semaphore_signal(barrier, inc=1, device_id=dev, device_id_type=MESH)

    with jax.named_scope("greet"):
        greet(e_dev)
        greet(w_dev)

        @pl.when(at_top)
        def _():
            greet(fold_dev)

        @pl.when(below_top)
        def _():
            greet(n_dev)

        @pl.when(inner)
        def _():
            greet(s_dev)

    load_kmt = pltpu.make_async_copy(kmt_ref, kmt_int, load_sem.at[pieces])
    load_kmt.start()
    loads = []
    for i in range(pieces):
        span = pl.ds(i * piece, piece)
        copy = pltpu.make_async_copy(x_ref.at[span], xv.at[span], load_sem.at[i])
        copy.start()
        loads.append(copy)
    flat = xv.reshape(tiles * rows, lanes)

    zeros = jnp.zeros((rows, lanes), jnp.float32)
    lane = lax.broadcasted_iota(jnp.int32, (rows, lanes), 1)
    row = lax.broadcasted_iota(jnp.int32, (rows, lanes), 0)
    spot = lane // QUAD
    part = lane // quad

    def pick(value, index):
        return jnp.take_along_axis(value, index, axis=1)

    def pack_quad(g):
        acc = zeros
        for q in range(quad):
            value = flat[pl.ds((g * quad + q) * rows, rows), :]
            value = pltpu.roll(value, (QUAD * q + QUAD // 2) % lanes, 1)
            acc = value if q == 0 else jnp.where(spot == q, value, acc)
        return acc

    def spread(group, off):
        index = QUAD * (lane % quad) + off
        acc = None
        for g, value in enumerate(group):
            value = pick(value, index)
            acc = value if g == 0 else jnp.where(part == g, value, acc)
        return acc

    def send(src, dst, s, r, dev):
        return pltpu.make_async_remote_copy(
            src_ref=src, dst_ref=dst, send_sem=send_sem.at[s], recv_sem=recv_sem.at[r],
            device_id=dev, device_id_type=MESH,
        )

    r_w, r_e = 4, 4 + regs
    first_row, last_row = xv.at[:, 0, :], xv.at[:, rows - 1, :]
    fold = [send(kmt_int, kmt_n, 0, 0, fold_dev), send(last_row, from_n, 1, 1, fold_dev)]
    to_n = [send(kmt_int, kmt_s, 0, 2, n_dev), send(last_row, from_s, 1, 3, n_dev)]
    to_s = [send(kmt_int, kmt_n, 2, 0, s_dev), send(first_row, from_n, 3, 1, s_dev)]
    to_e, to_w = [], []
    for j in range(regs):
        span = pl.ds(j * rows, rows)
        to_e.append(send(ecol.at[span], west.at[span], 4, r_w + j, e_dev))
        to_w.append(send(wcol.at[span], east.at[span], 5, r_e + j, w_dev))
    all_e = send(ecol, west, 4, r_w, e_dev)
    all_w = send(wcol, east, 5, r_e, w_dev)

    def send_rows(i):
        @pl.when(at_top)
        def _():
            fold[i].start()

        @pl.when(below_top)
        def _():
            to_n[i].start()

        @pl.when(inner)
        def _():
            to_s[i].start()

    packed = []

    def pack_reg(j):
        first, last = bounds[j] // quad, bounds[j + 1] // quad
        group = []
        for g in range(first, last):
            if g % per_piece == 0:
                loads[g // per_piece].wait()
            group.append(pack_quad(g))
        e, w = spread(group, 1), spread(group, 2)
        if j == 0:
            e = jnp.where(lane >= head, jnp.broadcast_to(kmt_own[:, lanes - 1 :], (rows, lanes)), e)
            w = jnp.where(lane >= head, jnp.broadcast_to(kmt_own[:, :1], (rows, lanes)), w)
        ecol[pl.ds(j * rows, rows), :] = e
        wcol[pl.ds(j * rows, rows), :] = w
        packed.append(group)

    with jax.named_scope("pack0"):
        load_kmt.wait()
        kmt_own = kmt_int[...].astype(jnp.float32)
        pack_reg(0)

    with jax.named_scope("barrier"):

        @pl.when(inner)
        def _():
            pl.semaphore_wait(barrier, 4)

        @pl.when(at_bottom)
        def _():
            pl.semaphore_wait(barrier, 3)

    with jax.named_scope("pack"):
        send_rows(0)
        to_e[0].start()
        to_w[0].start()
        for j in range(1, regs):
            pack_reg(j)
            to_e[j].start()
            to_w[j].start()
        send_rows(1)

    with jax.named_scope("inner"):
        for j in range(regs):
            inner_e[pl.ds(j * rows, rows), :] = spread(packed[j], 0)
            inner_w[pl.ds(j * rows, rows), :] = spread(packed[j], 3)

        @pl.when(at_bottom)
        def _():
            kmt_s[...] = jnp.zeros((rows, lanes), jnp.int32)
            for t in range(tracers):
                from_s[pl.ds(t * levels, levels), :] = jnp.zeros((levels, lanes), jnp.float32)

    def put(d, dk, k, value):
        coef[pl.ds(((d * 3 + dk) * levels + k) * rows, rows), :] = value

    def piece_of(d, dk, k):
        return coef[pl.ds(((d * 3 + dk) * levels + k) * rows, rows), :]

    with jax.named_scope("coefs"):
        none = jnp.zeros((1, rows, lanes), jnp.float32)

        def up3(v):
            return jnp.concatenate([none, v[:-1]], axis=0)

        def dn3(v):
            return jnp.concatenate([v[1:], none], axis=0)

        def shifted(v, by, axis):
            return jnp.stack([pltpu.roll(v[k], by, axis) for k in range(levels)])

        own_rho = jnp.stack(
            [HALINE * flat[pl.ds(plane + k * rows, rows), :] - THERMAL * flat[pl.ds(k * rows, rows), :]
             for k in range(levels)]
        )
        own_wet = jnp.stack([(kmt_own > float(k)).astype(jnp.float32) for k in range(levels)])
        c3 = column(own_rho, own_wet, up3, dn3)

        def moved(by, axis):
            return tuple(shifted(v, by, axis) for v in c3)

        mid_lane = jnp.logical_and(lane > 0, lane < lanes - 1)
        xc, xe, xw = line(c3, moved(lanes - 1, 1), moved(1, 1), up3, dn3)
        for dk in range(3):
            for k in range(levels):
                put(E, dk, k, jnp.where(mid_lane, xe[dk][k], 0.0))
                put(W, dk, k, jnp.where(mid_lane, xw[dk][k], 0.0))
                put(C, dk, k, jnp.where(mid_lane, xc[dk][k], 0.0))
        mid_row = jnp.logical_and(row > 0, row < rows - 1)
        yc, yn, ys = line(c3, moved(rows - 1, 0), moved(1, 0), up3, dn3)
        for dk in range(3):
            for k in range(levels):
                put(N, dk, k, jnp.where(mid_row, yn[dk][k], 0.0))
                put(S, dk, k, jnp.where(mid_row, ys[dk][k], 0.0))
                both = piece_of(C, dk, k) + jnp.where(mid_row, yc[dk][k], 0.0)
                put(C, dk, k, both + 1.0 if dk == 1 else both)

    with jax.named_scope("main"):

        @pl.loop(0, tracers // TOGETHER)
        def _(i):
            fields = []
            for u in range(TOGETHER):
                base = pl.multiple_of((i * TOGETHER + u) * plane, rows)
                field = []
                for k in range(levels):
                    own = flat[pl.ds(base + k * rows, rows), :]
                    field.append((
                        own, pltpu.roll(own, lanes - 1, 1), pltpu.roll(own, 1, 1),
                        pltpu.roll(own, rows - 1, 0), pltpu.roll(own, 1, 0),
                    ))
                fields.append(field)
            for k in range(levels):
                sums = [None] * TOGETHER
                for d in range(5):
                    for dk in range(3):
                        if not 0 <= k + dk - 1 < levels:
                            continue
                        c = piece_of(d, dk, k)
                        for u in range(TOGETHER):
                            term = c * fields[u][k + dk - 1][d]
                            sums[u] = term if sums[u] is None else sums[u] + term
                for u in range(TOGETHER):
                    base = pl.multiple_of((i * TOGETHER + u) * plane, rows)
                    out_ref[pl.ds(base + k * rows, rows), :] = sums[u]

    level = lax.broadcasted_iota(jnp.int32, (levels, lanes), 0)
    level_f = level.astype(jnp.float32)

    def up_s(v):
        return jnp.where(level == 0, 0.0, pltpu.roll(v, 1, 0))

    def dn_s(v):
        return jnp.where(level == levels - 1, 0.0, pltpu.roll(v, levels - 1, 0))

    def at_row(t, r):
        return flat[pl.ds(t * plane + r, levels, stride=rows), :]

    def row_column(t0, t1, kmt):
        wet = (jnp.broadcast_to(kmt, (levels, lanes)) > level_f).astype(jnp.float32)
        return column(HALINE * t1 - THERMAL * t0, wet, up_s, dn_s)

    def own_row(r):
        return row_column(at_row(0, r), at_row(1, r), kmt_own[r : r + 1, :])

    def fix_rows(source, kmt_row, r, r_in, north, turn):
        def halo(t):
            h = source[pl.ds(t * levels, levels), :]
            return pick(h, lanes - 1 - lane) if turn else h

        k = jnp.broadcast_to(kmt_row, (rows, lanes)).astype(jnp.float32)
        k = (pick(k, lanes - 1 - lane) if turn else k)[:1, :]
        out_c, in_c = row_column(halo(0), halo(1), k), own_row(r_in)
        p, m = (out_c, in_c) if north else (in_c, out_c)
        cc, cp, cm = line(own_row(r), p, m, up_s, dn_s)
        c_out, c_in = (cp, cm) if north else (cm, cp)
        table = (cc, c_out, c_in)
        lo = [pltpu.roll(c[0], levels - 1, 0) for c in table]
        mid = [c[1] for c in table]
        hi = [pltpu.roll(c[2], 1, 0) for c in table]

        @pl.loop(0, tracers // 8)
        def _(i):
            for u in range(8):
                t = i * 8 + u
                values = (at_row(t, r), halo(t), at_row(t, r_in))
                above = total([c * v for c, v in zip(lo, values)])
                same = total([c * v for c, v in zip(mid, values)])
                below = total([c * v for c, v in zip(hi, values)])
                place = pl.ds(t * plane + r, levels, stride=rows)
                out_ref[place, :] = (
                    out_ref[place, :] + same + pltpu.roll(above, 1, 0) + pltpu.roll(below, levels - 1, 0)
                )

    def fix_n(turn):
        for copy in fold:
            copy.wait_recv()
        at = rows - 1 if turn else 0
        fix_rows(from_n, kmt_n[at : at + 1, :], rows - 1, rows - 2, True, turn)

    with jax.named_scope("fixs"):

        @pl.when(inner)
        def _():
            for copy in to_n:
                copy.wait_recv()

        fix_rows(from_s, kmt_s[rows - 1 : rows, :], 0, 1, False, False)

    with jax.named_scope("fixn"):

        @pl.when(below_top)
        def _():
            fix_n(False)

    deep = lane % levels

    def up_l(v):
        return jnp.where(deep == 0, 0.0, pltpu.roll(v, 1, 1))

    def dn_l(v):
        return jnp.where(deep == levels - 1, 0.0, pltpu.roll(v, lanes - 1, 1))

    def lane_column(reg, kmt):
        rho = pick(HALINE * pltpu.roll(reg, lanes - levels, 1) - THERMAL * reg, deep)
        wet = (kmt > deep.astype(jnp.float32)).astype(jnp.float32)
        return column(rho, wet, up_l, dn_l)

    def own_kmt(at):
        return jnp.broadcast_to(kmt_own[:, at : at + 1], (rows, lanes))

    def reg_of(ref, j):
        return ref[pl.ds(j * rows, rows), :]

    def halo_column(ref):
        reg = reg_of(ref, 0)
        return lane_column(reg, jnp.broadcast_to(reg[:, head : head + 1], (rows, lanes)))

    with jax.named_scope("fixc"):
        ends = jnp.logical_or(lane == 0, lane == lanes - 1)
        even = lane % 2 == 0
        w_own = lane_column(reg_of(wcol, 0), own_kmt(0))
        w_in = lane_column(reg_of(inner_w, 0), own_kmt(1))
        e_own = lane_column(reg_of(ecol, 0), own_kmt(lanes - 1))
        e_in = lane_column(reg_of(inner_e, 0), own_kmt(lanes - 2))
        to_e[0].wait_recv()
        to_w[0].wait_recv()
        wc, wp, wm = line(w_own, w_in, halo_column(west), up_l, dn_l)
        ec, ep, em = line(e_own, halo_column(east), e_in, up_l, dn_l)

        def side(table, values):
            above = total([pltpu.roll(c[0], lanes - 1, 1) * v for c, v in zip(table, values)])
            same = total([c[1] * v for c, v in zip(table, values)])
            below = total([pltpu.roll(c[2], 1, 1) * v for c, v in zip(table, values)])
            return same + pltpu.roll(above, 1, 1) + pltpu.roll(below, lanes - 1, 1)

        for j in range(regs):
            if j:
                to_e[j].wait_recv()
                to_w[j].wait_recv()
            w = side((wc, wp, wm), (reg_of(wcol, j), reg_of(inner_w, j), reg_of(west, j)))
            e = side((ec, ep, em), (reg_of(ecol, j), reg_of(east, j), reg_of(inner_e, j)))
            e = pltpu.roll(e, lanes - 1, 1)
            mixed = (jnp.where(even, w, e), jnp.where(even, e, w))
            for q in range(bounds[j + 1] - bounds[j]):
                add = pltpu.roll(mixed[q % 2], (lanes - q) % lanes, 1)
                place = pl.ds((bounds[j] + q) * rows, rows)
                out_ref[place, :] = out_ref[place, :] + jnp.where(ends, add, 0.0)

    with jax.named_scope("fixtop"):

        @pl.when(at_top)
        def _():
            fix_n(True)

    with jax.named_scope("end"):
        for i in range(2):
            fold[i].wait_send()

            @pl.when(inner)
            def _():
                to_s[i].wait_send()

        all_e.wait_send()
        all_w.wait_send()


def solution(mesh):
    n_lon, n_lat = mesh.shape["lon"], mesh.shape["lat"]

    def local(tracers, kmt):
        nt, levels, rows, lanes = tracers.shape
        tiles = nt * levels
        regs = tiles // lanes + 1
        assert levels == rows and tiles % lanes and lanes % (tiles % lanes) == 0

        def vmem(*shape):
            return pltpu.VMEM(shape, jnp.float32)

        out = pl.pallas_call(
            functools.partial(kernel, (nt, levels, rows, lanes, n_lon, n_lat)),
            out_shape=pltpu.VMEM((tiles * rows, lanes), jnp.float32),
            in_specs=[pl.BlockSpec(memory_space=pltpu.HBM), pl.BlockSpec(memory_space=pltpu.HBM)],
            out_specs=pl.BlockSpec(memory_space=pltpu.VMEM),
            scratch_shapes=[
                vmem(tiles, rows, lanes),
                pltpu.VMEM((rows, lanes), jnp.int32),
                vmem(15 * levels * rows, lanes),
            ]
            + [vmem(regs * rows, lanes)] * 6
            + [vmem(tiles, lanes)] * 2
            + [pltpu.VMEM((rows, lanes), jnp.int32)] * 2
            + [
                pltpu.SemaphoreType.DMA((tiles // (tiles % lanes) + 1,)),
                pltpu.SemaphoreType.DMA((6,)),
                pltpu.SemaphoreType.DMA((4 + 2 * regs,)),
            ],
            compiler_params=pltpu.CompilerParams(collective_id=0, has_side_effects=True),
        )(tracers.reshape(tiles, rows, lanes), kmt)
        return out.reshape(nt, levels, rows, lanes)

    return jax.shard_map(
        local,
        mesh=mesh,
        in_specs=(P(None, None, "lat", "lon"), P("lat", "lon")),
        out_specs=P(None, None, "lat", "lon"),
        check_vma=False,
    )
```

profile of v0, /device:TPU:1, one launch (start us, length us, event | category | flops | bytes accessed | tf_op | source)
XLA Modules:
  0.0 14.1 jit_solution(7360117861663877912)
XLA Ops:
  0.0 13.0 %shard_map.28 = f32[2560,128]{1,0:T(8,128)S(1)} custom-call(f32[320,8,128]{2,1,0:T(8,128)} %bitcast.3, s32[8,128]{1,0:T(8,128)} %kmt_ref.1), custom_call_target="tpu_custom_call" | custom-call | tf_op jit(solution)/shard_map/pallas_call | solution.py:460
  13.0 1.1 %copy.4 = f32[40,8,8,128]{3,2,1,0:T(8,128)} copy(f32[40,8,8,128]{3,2,1,0:T(8,128)S(1)} %bitcast.2) | data formatting | bytes 2621440
where the time goes:
time: 14.3 us; the launch traced here: 14.1 us
  Pallas kernels  13 us (91%)
  local copies, waits for them, and re-layouts  1.06 us (7%)
    pallas_call x1, Pallas kernels, local(): pl.pallas_call(functools.partial(kernel, (nt, levels, rows, lanes, n_lon,...  13 us
    unnamed x1, local copies, waits for them, and re-layouts  1.06 us

commit v1 on v0

v1 whole, which is shorter than its diff:
```python
import functools

import jax
import jax.numpy as jnp
from jax import lax
from jax.experimental import pallas as pl
from jax.experimental.pallas import tpu as pltpu
from jax.sharding import PartitionSpec as P

THERMAL = 0.2
HALINE = 0.8
REDI = 0.1
SKEW = 0.05
SLOPE_MAX = 0.6
SLOPE_WIDTH = 0.2

MESH = pl.DeviceIdType.MESH
TOGETHER = 2
C, E, W, N, S = range(5)


def taper(slope):
    return slope * 0.5 * (1.0 + jnp.tanh((SLOPE_MAX - jnp.abs(slope)) / SLOPE_WIDTH))


def column(rho, wet, up, dn):
    hi = wet * dn(wet)
    strat = (dn(rho) - rho) * hi
    return rho, wet, hi, up(hi), 0.5 * (strat + up(strat))


def line(c, p, m, up, dn):
    c_rho, c_wet, c_hi, c_lo, c_cell = c
    p_rho, p_wet, p_hi, p_lo, p_cell = p
    m_rho, m_wet, m_hi, m_lo, m_cell = m
    mp, mm = c_wet * p_wet, c_wet * m_wet
    sp = taper((p_rho - c_rho) * mp / jnp.maximum(0.5 * (p_cell + c_cell), 1.0))
    sm = taper((c_rho - m_rho) * mm / jnp.maximum(0.5 * (m_cell + c_cell), 1.0))
    cx = 0.5 * (sp + sm)
    sw = 0.5 * (cx + dn(cx))
    fh = ((REDI + SKEW) * 0.25) * sw * c_hi
    zh = REDI * (sw * sw) * c_hi
    fl, zl = up(fh), up(zh)
    pp = ((REDI - SKEW) * 0.25) * sp * mp
    pm = -((REDI - SKEW) * 0.25) * sm * mm
    own_p, own_m = mp * (fh - fl), mm * (fl - fh)
    mph, mmh = dn(mp) * fh, dn(mm) * fh
    mpl, mml = up(mp) * fl, up(mm) * fl
    q = pp + pm
    return (
        (mpl - mml - q * c_lo + zl,
         q * (c_lo - c_hi) - REDI * (mp + mm) - (own_p + own_m) - (zh + zl),
         mmh - mph + q * c_hi + zh),
        (-pp * p_lo - mpl, REDI * mp + pp * (p_lo - p_hi) + own_p, pp * p_hi + mph),
        (mml - pm * m_lo, REDI * mm + pm * (m_lo - m_hi) + own_m, pm * m_hi - mmh),
    )


def total(terms):
    result = terms[0]
    for term in terms[1:]:
        result = result + term
    return result


def kernel(
    sizes, x_ref, kmt_ref, out_ref,
    xv, kmt_int, coef, wcol, ecol, inner_w, inner_e, west, east, relay, from_n, from_s,
    load_sem, send_sem, recv_sem,
):
    tracers, levels, rows, lanes, n_lon, n_lat, pieces = sizes
    lon, lat = lax.axis_index("lon"), lax.axis_index("lat")
    at_top = lat == n_lat - 1
    below_top = jnp.logical_not(at_top)
    inner = lat > 0
    at_bottom = jnp.logical_not(inner)
    even_lat = lat < 0
    odd_lat = lat < 0
    relayed = jnp.logical_and(lon == 0, even_lat)
    relays = jnp.logical_and(lon == 0, odd_lat)
    far = jnp.logical_and(lon == n_lon - 1, even_lat)
    direct, near = jnp.logical_not(relayed), jnp.logical_not(far)
    early = jnp.logical_and(lon == 0, direct)
    late = jnp.logical_not(early)
    late_top, late_below = jnp.logical_and(late, at_top), jnp.logical_and(late, below_top)
    e_dev = (lax.rem(lon + 1, n_lon), lat)
    w_dev = (lax.rem(lon + n_lon - 1, n_lon), lat)
    n_dev, s_dev = (lon, lat + 1), (lon, lat - 1)
    fold_dev = (n_lon - 1 - lon, lat)
    tiles = tracers * levels
    plane = levels * rows
    group = tracers // pieces
    piece = group * levels
    slot = tracers + 2
    per = (lanes - 2) // slot
    regs = (levels + per - 1) // per

    barrier = pltpu.get_barrier_semaphore()

    def greet(dev):
        pl.semaphore_signal(barrier, inc=1, device_id=dev, device_id_type=MESH)

    with jax.named_scope("greet"):
        greet(w_dev)

        @pl.when(near)
        def _():
            greet(e_dev)

        @pl.when(far)
        def _():
            greet((0, lat + 1))

        @pl.when(at_top)
        def _():
            greet(fold_dev)

        @pl.when(below_top)
        def _():
            greet(n_dev)

        @pl.when(inner)
        def _():
            greet(s_dev)

    load_kmt = pltpu.make_async_copy(kmt_ref, kmt_int, load_sem.at[pieces])
    load_kmt.start()
    loads = []
    for i in range(pieces):
        span = pl.ds(i * piece, piece)
        copy = pltpu.make_async_copy(x_ref.at[span], xv.at[span], load_sem.at[i])
        copy.start()
        loads.append(copy)
    flat = xv.reshape((tiles + 1) * rows, lanes)

    lane = lax.broadcasted_iota(jnp.int32, (rows, lanes), 1)
    row = lax.broadcasted_iota(jnp.int32, (rows, lanes), 0)

    def pick(value, index):
        return jnp.take_along_axis(value, index, axis=1)

    def send(src, dst, s, r, dev):
        return pltpu.make_async_remote_copy(
            src_ref=src, dst_ref=dst, send_sem=send_sem.at[s], recv_sem=recv_sem.at[r],
            device_id=dev, device_id_type=MESH,
        )

    def rows_of(r, span, dst, s, dev):
        return send(xv.at[span, r, :], dst.at[span], s, s, dev)

    every = pl.ds(0, tiles + 1)
    fold = rows_of(rows - 1, every, from_n, 0, fold_dev)
    to_n = send(xv.at[every, rows - 1, :], from_s.at[every], 0, 1, n_dev)
    to_s = send(xv.at[every, 0, :], from_n.at[every], 1, 0, s_dev)
    cuts = [i * piece for i in range(pieces)] + [tiles + 1]
    folds = [
        rows_of(rows - 1, pl.ds(cuts[i], cuts[i + 1] - cuts[i]), from_n, 0, fold_dev) for i in range(pieces)
    ]
    to_e = send(ecol, west, 2, 2, e_dev)
    to_w = send(wcol, east, 3, 3, w_dev)
    to_relay = send(wcol, relay, 3, 4, n_dev)
    onward = send(relay, east, 4, 3, (n_lon - 1, lat - 1))

    def tile(t, k):
        return flat[pl.ds(t * plane + k * rows, rows), :]

    def density(k):
        return HALINE * tile(1, k) - THERMAL * tile(0, k)

    def gather_columns(e_ref, w_ref, e_off, w_off, before=None):
        zeros = jnp.zeros((rows, lanes), jnp.float32)
        es, ws = [zeros] * regs, [zeros] * regs

        def place(value, at, reg):
            value = pltpu.roll(value, at + 1, 1)
            es[reg] = jnp.where(lane == (at + e_off) % lanes, value, es[reg])
            ws[reg] = jnp.where(lane == (at + w_off) % lanes, value, ws[reg])

        for i in range(pieces):
            if before is not None:
                before(i)
            if i == 0:
                place(kmt_own, per * slot, 0)
                for k in range(levels):
                    place(density(k), k % per * slot + tracers, k // per)
            for t in range(i * group, (i + 1) * group):
                for k in range(levels):
                    place(tile(t, k), k % per * slot + t, k // per)
        for j in range(regs):
            e_ref[pl.ds(j * rows, rows), :] = es[j]
            w_ref[pl.ds(j * rows, rows), :] = ws[j]

    def enter():
        @pl.when(at_bottom)
        def _():
            pl.semaphore_wait(barrier, 3)

        @pl.when(jnp.logical_and(inner, jnp.logical_not(jnp.logical_or(relayed, relays))))
        def _():
            pl.semaphore_wait(barrier, 4)

        @pl.when(relayed)
        def _():
            pl.semaphore_wait(barrier, 3)

        @pl.when(relays)
        def _():
            pl.semaphore_wait(barrier, 5)

    def send_inner_rows():
        @pl.when(below_top)
        def _():
            to_n.start()

        @pl.when(inner)
        def _():
            to_s.start()

    held = max(pieces - 2, 1)

    def before(i):
        with jax.named_scope(f"load{i}"):
            loads[i].wait()
        if i == 0:

            @pl.when(late_top)
            def _():
                enter()

        if i < held:

            @pl.when(late_top)
            def _():
                folds[i].start()

        if i == pieces - 1:

            @pl.when(late_below)
            def _():
                with jax.named_scope("barrier"):
                    enter()

            @pl.when(late)
            def _():
                send_inner_rows()

    with jax.named_scope("loadk"):
        load_kmt.wait()
    kmt_own = kmt_int[...].astype(jnp.float32)
    xv[tiles, :, :] = kmt_own
    gather_columns(ecol, wcol, 0, 1, before)
    with jax.named_scope("send"):

        @pl.when(late)
        def _():
            to_e.start()

        @pl.when(jnp.logical_and(late, direct))
        def _():
            to_w.start()

        @pl.when(relayed)
        def _():
            to_relay.start()

        @pl.when(late_top)
        def _():
            for i in range(held, pieces):
                folds[i].start()

    with jax.named_scope("inner"):
        gather_columns(inner_e, inner_w, -1, 2)

        @pl.when(at_bottom)
        def _():
            for t in range(tracers + 1):
                from_s[pl.ds(t * levels, levels), :] = jnp.zeros((levels, lanes), jnp.float32)

    def put(d, dk, k, value):
        coef[pl.ds(((d * 3 + dk) * levels + k) * rows, rows), :] = value

    def piece_of(d, dk, k):
        return coef[pl.ds(((d * 3 + dk) * levels + k) * rows, rows), :]

    with jax.named_scope("coefs"):
        none = jnp.zeros((1, rows, lanes), jnp.float32)

        def up3(v):
            return jnp.concatenate([none, v[:-1]], axis=0)

        def dn3(v):
            return jnp.concatenate([v[1:], none], axis=0)

        def shifted(v, by, axis):
            return jnp.stack([pltpu.roll(v[k], by, axis) for k in range(levels)])

        own_rho = jnp.stack([density(k) for k in range(levels)])
        own_wet = jnp.stack([(kmt_own > float(k)).astype(jnp.float32) for k in range(levels)])
        c3 = column(own_rho, own_wet, up3, dn3)

        def moved(by, axis):
            return tuple(shifted(v, by, axis) for v in c3)

        mid_lane = jnp.logical_and(lane > 0, lane < lanes - 1)
        xc, xe, xw = line(c3, moved(lanes - 1, 1), moved(1, 1), up3, dn3)
        for dk in range(3):
            for k in range(levels):
                put(E, dk, k, jnp.where(mid_lane, xe[dk][k], 0.0))
                put(W, dk, k, jnp.where(mid_lane, xw[dk][k], 0.0))
                put(C, dk, k, jnp.where(mid_lane, xc[dk][k], 0.0))
        mid_row = jnp.logical_and(row > 0, row < rows - 1)
        yc, yn, ys = line(c3, moved(rows - 1, 0), moved(1, 0), up3, dn3)
        for dk in range(3):
            for k in range(levels):
                put(N, dk, k, jnp.where(mid_row, yn[dk][k], 0.0))
                put(S, dk, k, jnp.where(mid_row, ys[dk][k], 0.0))
                both = piece_of(C, dk, k) + jnp.where(mid_row, yc[dk][k], 0.0)
                put(C, dk, k, both + 1.0 if dk == 1 else both)

    with jax.named_scope("main"):

        @pl.loop(0, tracers // TOGETHER)
        def _(i):
            fields = []
            for u in range(TOGETHER):
                base = pl.multiple_of((i * TOGETHER + u) * plane, rows)
                field = []
                for k in range(levels):
                    own = flat[pl.ds(base + k * rows, rows), :]
                    field.append((
                        own, pltpu.roll(own, lanes - 1, 1), pltpu.roll(own, 1, 1),
                        pltpu.roll(own, rows - 1, 0), pltpu.roll(own, 1, 0),
                    ))
                fields.append(field)
            for k in range(levels):
                sums = [None] * TOGETHER
                for d in range(5):
                    for dk in range(3):
                        if not 0 <= k + dk - 1 < levels:
                            continue
                        c = piece_of(d, dk, k)
                        for u in range(TOGETHER):
                            term = c * fields[u][k + dk - 1][d]
                            sums[u] = term if sums[u] is None else sums[u] + term
                for u in range(TOGETHER):
                    base = pl.multiple_of((i * TOGETHER + u) * plane, rows)
                    out_ref[pl.ds(base + k * rows, rows), :] = sums[u]

    @pl.when(early)
    def _():
        with jax.named_scope("barrier"):
            enter()
        to_e.start()
        to_w.start()
        send_inner_rows()

        @pl.when(at_top)
        def _():
            fold.start()

    @pl.when(relays)
    def _():
        to_relay.wait_recv()
        onward.start()

    level = lax.broadcasted_iota(jnp.int32, (levels, lanes), 0)
    level_f = level.astype(jnp.float32)

    def up_s(v):
        return jnp.where(level == 0, 0.0, pltpu.roll(v, 1, 0))

    def dn_s(v):
        return jnp.where(level == levels - 1, 0.0, pltpu.roll(v, levels - 1, 0))

    def at_row(t, r):
        return flat[pl.ds(t * plane + r, levels, stride=rows), :]

    def row_column(t0, t1, kmt):
        wet = (jnp.broadcast_to(kmt, (levels, lanes)) > level_f).astype(jnp.float32)
        return column(HALINE * t1 - THERMAL * t0, wet, up_s, dn_s)

    def own_row(r):
        return row_column(at_row(0, r), at_row(1, r), kmt_own[r : r + 1, :])

    def fix_rows(source, r, r_in, north, turn):
        def halo(t):
            h = source[pl.ds(t * levels, levels), :]
            return pick(h, lanes - 1 - lane) if turn else h

        k = halo(tracers)[:1, :]
        out_c, in_c = row_column(halo(0), halo(1), k), own_row(r_in)
        p, m = (out_c, in_c) if north else (in_c, out_c)
        cc, cp, cm = line(own_row(r), p, m, up_s, dn_s)
        c_out, c_in = (cp, cm) if north else (cm, cp)
        table = (cc, c_out, c_in)
        lo = [pltpu.roll(c[0], levels - 1, 0) for c in table]
        mid = [c[1] for c in table]
        hi = [pltpu.roll(c[2], 1, 0) for c in table]

        batch = tracers // 2 if turn else group

        @pl.loop(0, tracers // batch)
        def _(i):
            for u in range(batch):
                t = i * batch + u
                values = (at_row(t, r), halo(t), at_row(t, r_in))
                above = total([c * v for c, v in zip(lo, values)])
                same = total([c * v for c, v in zip(mid, values)])
                below = total([c * v for c, v in zip(hi, values)])
                place = pl.ds(t * plane + r, levels, stride=rows)
                out_ref[place, :] = (
                    out_ref[place, :] + same + pltpu.roll(above, 1, 0) + pltpu.roll(below, levels - 1, 0)
                )

    def fix_n(turn):
        fold.wait_recv()
        fix_rows(from_n, rows - 1, rows - 2, True, turn)

    with jax.named_scope("fixs"):

        @pl.when(inner)
        def _():
            to_n.wait_recv()

        fix_rows(from_s, 0, 1, False, False)

    with jax.named_scope("fixn"):

        @pl.when(below_top)
        def _():
            fix_n(False)

    west_side = lane % 2 == 0
    spot = jnp.minimum((lane + 1) // 2 % (lanes // 2), tracers - 1)

    def both(w_ref, e_ref, w_off, e_off, at, k):
        base, span = k % per * slot, pl.ds(k // per * rows, rows)
        w_at = (base + at + w_off + lanes) % lanes
        e_at = (base + at + e_off + lanes) % lanes
        return jnp.where(west_side, pick(w_ref[span, :], w_at), pick(e_ref[span, :], e_at))

    def edge(w_ref, e_ref, w_off, e_off):
        args = (w_ref, e_ref, w_off, e_off)
        fixed = jnp.full((rows, lanes), tracers, jnp.int32)
        values = jnp.stack([both(*args, spot, k) for k in range(levels)])
        rho = jnp.stack([both(*args, fixed, k) for k in range(levels)])
        kmt = both(*args, jnp.full((rows, lanes), per * slot, jnp.int32), 0)
        wet = jnp.stack([(kmt > float(k)).astype(jnp.float32) for k in range(levels)])
        return values, column(rho, wet, up3, dn3)

    with jax.named_scope("fixc0"):
        own, own_c = edge(wcol, ecol, 1, 0)
        ins, ins_c = edge(inner_w, inner_e, 2, -1)
    with jax.named_scope("waitc"):
        to_e.wait_recv()
        to_w.wait_recv()
    with jax.named_scope("fixc1"):
        outs, outs_c = edge(west, east, 0, 1)
        table = line(own_c, outs_c, ins_c, up3, dn3)
        values = (own, outs, ins)
        above = total([c[0] * up3(v) for c, v in zip(table, values)])
        same = total([c[1] * v for c, v in zip(table, values)])
        below = total([c[2] * dn3(v) for c, v in zip(table, values)])
        add = same + above + below
        ends = jnp.logical_or(lane == 0, lane == lanes - 1)
        for t in range(tracers):
            for k in range(levels):
                term = pltpu.roll(add[k], (lanes - 2 * t) % lanes, 1)
                place = pl.ds(t * plane + k * rows, rows)
                out_ref[place, :] = out_ref[place, :] + jnp.where(ends, term, 0.0)

    with jax.named_scope("fixtop"):

        @pl.when(at_top)
        def _():
            fix_n(True)

    with jax.named_scope("end"):
        fold.wait_send()

        @pl.when(inner)
        def _():
            to_s.wait_send()

        to_e.wait_send()
        to_w.wait_send()

        @pl.when(relays)
        def _():
            onward.wait_send()


def solution(mesh):
    n_lon, n_lat = mesh.shape["lon"], mesh.shape["lat"]

    def local(tracers, kmt):
        nt, levels, rows, lanes = tracers.shape
        tiles = nt * levels
        per = (lanes - 2) // (nt + 2)
        regs = (levels + per - 1) // per
        pieces = 5 if nt % 5 == 0 else 1
        assert levels == rows and per > 0

        def vmem(*shape):
            return pltpu.VMEM(shape, jnp.float32)

        out = pl.pallas_call(
            functools.partial(kernel, (nt, levels, rows, lanes, n_lon, n_lat, pieces)),
            out_shape=pltpu.VMEM((tiles * rows, lanes), jnp.float32),
            in_specs=[pl.BlockSpec(memory_space=pltpu.HBM), pl.BlockSpec(memory_space=pltpu.HBM)],
            out_specs=pl.BlockSpec(memory_space=pltpu.VMEM),
            scratch_shapes=[
                vmem(tiles + 1, rows, lanes),
                pltpu.VMEM((rows, lanes), jnp.int32),
                vmem(15 * levels * rows, lanes),
            ]
            + [vmem(regs * rows, lanes)] * 7
            + [vmem(tiles + rows, lanes)] * 2
            + [
                pltpu.SemaphoreType.DMA((pieces + 1,)),
                pltpu.SemaphoreType.DMA((5,)),
                pltpu.SemaphoreType.DMA((5,)),
            ],
            compiler_params=pltpu.CompilerParams(collective_id=0, has_side_effects=True),
        )(tracers.reshape(tiles, rows, lanes), kmt)
        return out.reshape(nt, levels, rows, lanes)

    return jax.shard_map(
        local,
        mesh=mesh,
        in_specs=(P(None, None, "lat", "lon"), P("lat", "lon")),
        out_specs=P(None, None, "lat", "lon"),
        check_vma=False,
    )
```

time: 14.3 us -> 12.9 us (0.902)
  Pallas kernels: 13 us -> 11.7 us
    pallas_call x1, Pallas kernels: 13 us -> 11.7 us  [local(): pl.pallas_call(functools.partial(kernel, (nt, levels, rows, lanes, n_lon,...]
where the time goes in v1:
time: 12.9 us; the launch traced here: 12.7 us
  Pallas kernels  11.7 us (91%)
  local copies, waits for them, and re-layouts  1.06 us (8%)
    pallas_call x1, Pallas kernels, local(): pl.pallas_call(functools.partial(kernel, (nt, levels, rows, lanes, n_lon,...  11.7 us
    unnamed x1, local copies, waits for them, and re-layouts  1.06 us

profile of v1, /device:TPU:1, one launch (start us, length us, event | category | flops | bytes accessed | tf_op | source)
XLA Modules:
  0.0 12.7 jit_solution(5626733271170175137)
XLA Ops:
  0.0 11.7 %shard_map.28 = f32[2560,128]{1,0:T(8,128)S(1)} custom-call(f32[320,8,128]{2,1,0:T(8,128)} %bitcast.3, s32[8,128]{1,0:T(8,128)} %kmt_ref.1), custom_call_target="tpu_custom_call" | custom-call | tf_op jit(solution)/shard_map/pallas_call | solution.py:507
  11.7 1.1 %copy.4 = f32[40,8,8,128]{3,2,1,0:T(8,128)} copy(f32[40,8,8,128]{3,2,1,0:T(8,128)S(1)} %bitcast.2) | data formatting | bytes 2621440

commit v2 on v1

--- a/solution.py
+++ b/solution.py
@@ -74,8 +74,8 @@
     below_top = jnp.logical_not(at_top)
     inner = lat > 0
     at_bottom = jnp.logical_not(inner)
-    even_lat = lat < 0
-    odd_lat = lat < 0
+    even_lat = jnp.logical_and(inner, jnp.logical_and(lat % 2 == 0, below_top))
+    odd_lat = jnp.logical_and(lat > 1, lat % 2 == 1)
     relayed = jnp.logical_and(lon == 0, even_lat)
     relays = jnp.logical_and(lon == 0, odd_lat)
     far = jnp.logical_and(lon == n_lon - 1, even_lat)
@@ -86,6 +86,7 @@
     e_dev = (lax.rem(lon + 1, n_lon), lat)
     w_dev = (lax.rem(lon + n_lon - 1, n_lon), lat)
     n_dev, s_dev = (lon, lat + 1), (lon, lat - 1)
+    lat_up, lat_down = lax.rem(lat + 1, n_lat), lax.rem(lat + n_lat - 1, n_lat)
     fold_dev = (n_lon - 1 - lon, lat)
     tiles = tracers * levels
     plane = levels * rows
@@ -109,7 +110,7 @@
 
         @pl.when(far)
         def _():
-            greet((0, lat + 1))
+            greet((0, lat_up))
 
         @pl.when(at_top)
         def _():
@@ -158,8 +159,8 @@
     ]
     to_e = send(ecol, west, 2, 2, e_dev)
     to_w = send(wcol, east, 3, 3, w_dev)
-    to_relay = send(wcol, relay, 3, 4, n_dev)
-    onward = send(relay, east, 4, 3, (n_lon - 1, lat - 1))
+    to_relay = send(wcol, relay, 3, 4, (lon, lat_up))
+    onward = send(relay, east, 4, 3, (n_lon - 1, lat_down))
 
     def tile(t, k):
         return flat[pl.ds(t * plane + k * rows, rows), :]

time: 12.9 us -> 11.4 us (0.88)
  the two profiles are of different devices: /device:TPU:1 before, /device:TPU:0 now
where the time goes in v2:
time: 11.4 us; the launch traced here: 11.2 us
  Pallas kernels  10.2 us (89%)
  local copies, waits for them, and re-layouts  1.06 us (9%)
    pallas_call x1, Pallas kernels, local(): pl.pallas_call(functools.partial(kernel, (nt, levels, rows, lanes, n_lon,...  10.2 us
    unnamed x1, local copies, waits for them, and re-layouts  1.06 us

profile of v2, /device:TPU:0, one launch (start us, length us, event | category | flops | bytes accessed | tf_op | source)
XLA Modules:
  0.0 11.2 jit_solution(5745558102486772859)
XLA Ops:
  0.0 10.2 %shard_map.28 = f32[2560,128]{1,0:T(8,128)S(1)} custom-call(f32[320,8,128]{2,1,0:T(8,128)} %bitcast.3, s32[8,128]{1,0:T(8,128)} %kmt_ref.1), custom_call_target="tpu_custom_call" | custom-call | tf_op jit(solution)/shard_map/pallas_call | solution.py:508
  10.2 1.1 %copy.4 = f32[40,8,8,128]{3,2,1,0:T(8,128)} copy(f32[40,8,8,128]{3,2,1,0:T(8,128)S(1)} %bitcast.2) | data formatting | bytes 2621440

commit v3 on v2

--- a/solution.py
+++ b/solution.py
@@ -64,7 +64,7 @@
 
 
 def kernel(
-    sizes, x_ref, kmt_ref, out_ref,
+    sizes, x_ref, kmt_ref, out_ref, add_ref,
     xv, kmt_int, coef, wcol, ecol, inner_w, inner_e, west, east, relay, from_n, from_s,
     load_sem, send_sem, recv_sem,
 ):
@@ -168,6 +168,11 @@
     def density(k):
         return HALINE * tile(1, k) - THERMAL * tile(0, k)
 
+    starts = {0: 1}
+    while max(starts.values()) < pieces:
+        last = max(starts.values())
+        starts[last] = min(last + 2, pieces)
+
     def gather_columns(e_ref, w_ref, e_off, w_off, before=None):
         zeros = jnp.zeros((rows, lanes), jnp.float32)
         es, ws = [zeros] * regs, [zeros] * regs
@@ -178,8 +183,9 @@
             ws[reg] = jnp.where(lane == (at + w_off) % lanes, value, ws[reg])
 
         for i in range(pieces):
-            if before is not None:
-                before(i)
+            if before is not None and i in starts:
+                for n in range(i, starts[i]):
+                    before(n)
             if i == 0:
                 place(kmt_own, per * slot, 0)
                 for k in range(levels):
@@ -462,13 +468,8 @@
         above = total([c[0] * up3(v) for c, v in zip(table, values)])
         same = total([c[1] * v for c, v in zip(table, values)])
         below = total([c[2] * dn3(v) for c, v in zip(table, values)])
-        add = same + above + below
-        ends = jnp.logical_or(lane == 0, lane == lanes - 1)
-        for t in range(tracers):
-            for k in range(levels):
-                term = pltpu.roll(add[k], (lanes - 2 * t) % lanes, 1)
-                place = pl.ds(t * plane + k * rows, rows)
-                out_ref[place, :] = out_ref[place, :] + jnp.where(ends, term, 0.0)
+        for k in range(levels):
+            add_ref[pl.ds(k * rows, rows), :] = same[k] + above[k] + below[k]
 
     with jax.named_scope("fixtop"):
 
@@ -489,6 +490,30 @@
         @pl.when(relays)
         def _():
             onward.wait_send()
+
+
+def finish(sizes, part_ref, add_ref, out_ref, stage, sem):
+    tracers, levels, rows, lanes, pieces = sizes
+    plane = levels * rows
+    group = tracers // pieces
+    lane = lax.broadcasted_iota(jnp.int32, (rows, lanes), 1)
+    ends = jnp.logical_or(lane == 0, lane == lanes - 1)
+    add = [add_ref[pl.ds(k * rows, rows), :] for k in range(levels)]
+    copies = []
+    for i in range(pieces):
+        with jax.named_scope(f"insert{i}"):
+            for t in range(i * group, (i + 1) * group):
+                for k in range(levels):
+                    term = pltpu.roll(add[k], (lanes - 2 * t) % lanes, 1)
+                    place = pl.ds(t * plane + k * rows, rows)
+                    stage[place, :] = part_ref[place, :] + jnp.where(ends, term, 0.0)
+            span = pl.ds(i * group * plane, group * plane)
+            copy = pltpu.make_async_copy(stage.at[span], out_ref.at[span], sem.at[i])
+            copy.start()
+            copies.append(copy)
+    with jax.named_scope("written"):
+        for copy in copies:
+            copy.wait()
 
 
 def solution(mesh):
@@ -505,11 +530,11 @@
         def vmem(*shape):
             return pltpu.VMEM(shape, jnp.float32)
 
-        out = pl.pallas_call(
+        part, add = pl.pallas_call(
             functools.partial(kernel, (nt, levels, rows, lanes, n_lon, n_lat, pieces)),
-            out_shape=pltpu.VMEM((tiles * rows, lanes), jnp.float32),
+            out_shape=[vmem(tiles * rows, lanes), vmem(levels * rows, lanes)],
             in_specs=[pl.BlockSpec(memory_space=pltpu.HBM), pl.BlockSpec(memory_space=pltpu.HBM)],
-            out_specs=pl.BlockSpec(memory_space=pltpu.VMEM),
+            out_specs=[pl.BlockSpec(memory_space=pltpu.VMEM)] * 2,
             scratch_shapes=[
                 vmem(tiles + 1, rows, lanes),
                 pltpu.VMEM((rows, lanes), jnp.int32),
@@ -524,6 +549,14 @@
             ],
             compiler_params=pltpu.CompilerParams(collective_id=0, has_side_effects=True),
         )(tracers.reshape(tiles, rows, lanes), kmt)
+        part, add = (pltpu.with_memory_space_constraint(v, pltpu.VMEM) for v in (part, add))
+        out = pl.pallas_call(
+            functools.partial(finish, (nt, levels, rows, lanes, pieces)),
+            out_shape=jax.ShapeDtypeStruct((tiles * rows, lanes), jnp.float32),
+            in_specs=[pl.BlockSpec(memory_space=pltpu.VMEM)] * 2,
+            out_specs=pl.BlockSpec(memory_space=pltpu.HBM),
+            scratch_shapes=[vmem(tiles * rows, lanes), pltpu.SemaphoreType.DMA((pieces,))],
+        )(part, add)
         return out.reshape(nt, levels, rows, lanes)
 
     return jax.shard_map(

time: 11.4 us -> 11 us (0.965)
  local copies, waits for them, and re-layouts: 1.06 us -> 0 us
  Pallas kernels: 10.2 us -> 10.8 us
    pallas_call x0 -> x1, Pallas kernels: none -> 1.22 us  [local(): pl.pallas_call(functools.partial(finish, (nt, levels, rows, lanes, pieces...]
    unnamed x1 -> x0, local copies, waits for them, and re-layouts: 1.06 us -> none
    pallas_call x1, Pallas kernels: 10.2 us -> 9.57 us  [local(): pl.pallas_call(functools.partial(kernel, (nt, levels, rows, lanes, n_lon,...]
where the time goes in v3:
time: 11 us; the launch traced here: 10.8 us
  Pallas kernels  10.8 us (98%)
    pallas_call x1, Pallas kernels, local(): pl.pallas_call(functools.partial(kernel, (nt, levels, rows, lanes, n_lon,...  9.57 us
    pallas_call x1, Pallas kernels, local(): pl.pallas_call(functools.partial(finish, (nt, levels, rows, lanes, pieces...  1.22 us

profile of v3, /device:TPU:0, one launch (start us, length us, event | category | flops | bytes accessed | tf_op | source)
XLA Modules:
  0.0 10.8 jit_solution(10889870684666009385)
XLA Ops:
  0.0 9.6 %shard_map.28 = (f32[2560,128]{1,0:T(8,128)S(1)}, f32[64,128]{1,0:T(8,128)S(1)}) custom-call(f32[320,8,128]{2,1,0:T(8,128)} %bitcast.2, s32[8,128]{1,0:T(8,128)} %kmt_ref.1), custom_call_target="tpu_custom_call" | custom-call | tf_op jit(solution)/shard_map/pallas_call | solution.py:533
  9.6 1.2 %shard_map.29 = f32[2560,128]{1,0:T(8,128)} custom-call(f32[2560,128]{1,0:T(8,128)S(1)} %get-tuple-element.7.part_ref, f32[64,128]{1,0:T(8,128)S(1)} %get-tuple-element.8.add_ref), custom_call_target="tpu_custom_call" | custom-call | tf_op jit(solution)/shard_map/pallas_call | solution.py:553

commit v4 on v3

--- a/solution.py
+++ b/solution.py
@@ -16,6 +16,7 @@
 
 MESH = pl.DeviceIdType.MESH
 TOGETHER = 2
+STORE = 2
 C, E, W, N, S = range(5)
 
 
@@ -63,12 +64,20 @@
     return result
 
 
-def kernel(
+def kernel(sizes, x_ref, kmt_ref, out_ref, add_ref, *scratch):
+    pl.run_scoped(
+        functools.partial(body, sizes, x_ref, kmt_ref, out_ref, add_ref, *scratch),
+        pltpu.SemaphoreType.DMA((len(sizes[-1]) + 1,)),
+        pltpu.SemaphoreType.DMA((5,)),
+    )
+
+
+def body(
     sizes, x_ref, kmt_ref, out_ref, add_ref,
     xv, kmt_int, coef, wcol, ecol, inner_w, inner_e, west, east, relay, from_n, from_s,
-    load_sem, send_sem, recv_sem,
+    recv_sem, load_sem, send_sem,
 ):
-    tracers, levels, rows, lanes, n_lon, n_lat, pieces = sizes
+    tracers, levels, rows, lanes, n_lon, n_lat, groups = sizes
     lon, lat = lax.axis_index("lon"), lax.axis_index("lat")
     at_top = lat == n_lat - 1
     below_top = jnp.logical_not(at_top)
@@ -90,8 +99,8 @@
     fold_dev = (n_lon - 1 - lon, lat)
     tiles = tracers * levels
     plane = levels * rows
-    group = tracers // pieces
-    piece = group * levels
+    lead = levels
+    ends = [sum(groups[:i]) for i in range(len(groups) + 1)]
     slot = tracers + 2
     per = (lanes - 2) // slot
     regs = (levels + per - 1) // per
@@ -124,15 +133,19 @@
         def _():
             greet(s_dev)
 
-    load_kmt = pltpu.make_async_copy(kmt_ref, kmt_int, load_sem.at[pieces])
+    load_kmt = pltpu.make_async_copy(kmt_ref, kmt_int, load_sem.at[len(groups)])
     load_kmt.start()
-    loads = []
-    for i in range(pieces):
-        span = pl.ds(i * piece, piece)
-        copy = pltpu.make_async_copy(x_ref.at[span], xv.at[span], load_sem.at[i])
-        copy.start()
-        loads.append(copy)
-    flat = xv.reshape((tiles + 1) * rows, lanes)
+
+    def load(first, count, i):
+        return pltpu.make_async_copy(
+            x_ref.at[pl.ds(first, count)], xv.at[pl.ds(lead + first, count)], load_sem.at[i]
+        )
+
+    for i in range(len(groups)):
+        for t in range(ends[i], ends[i + 1]):
+            load(t * levels, levels, i).start()
+    loads = [load(ends[i] * levels, groups[i] * levels, i) for i in range(len(groups))]
+    flat = xv.reshape((lead + tiles) * rows, lanes)
 
     lane = lax.broadcasted_iota(jnp.int32, (rows, lanes), 1)
     row = lax.broadcasted_iota(jnp.int32, (rows, lanes), 0)
@@ -146,32 +159,32 @@
             device_id=dev, device_id_type=MESH,
         )
 
-    def rows_of(r, span, dst, s, dev):
-        return send(xv.at[span, r, :], dst.at[span], s, s, dev)
-
-    every = pl.ds(0, tiles + 1)
-    fold = rows_of(rows - 1, every, from_n, 0, fold_dev)
-    to_n = send(xv.at[every, rows - 1, :], from_s.at[every], 0, 1, n_dev)
-    to_s = send(xv.at[every, 0, :], from_n.at[every], 1, 0, s_dev)
-    cuts = [i * piece for i in range(pieces)] + [tiles + 1]
+    def rows_of(r, span, dst, s, into, dev):
+        return send(xv.at[span, r, :], dst.at[span], s, into, dev)
+
+    cut = lead + ends[-2] * levels
+    starts = [lead - 1] + [lead + e * levels for e in ends[1:]]
+    spans = [pl.ds(a, b - a) for a, b in zip(starts, starts[1:])]
+    every = pl.ds(lead - 1, tiles + 1)
+    halves = [(pl.ds(lead - 1, cut - lead + 1), 0), (spans[-1], 5)]
+    fold = rows_of(rows - 1, every, from_n, 0, 0, fold_dev)
     folds = [
-        rows_of(rows - 1, pl.ds(cuts[i], cuts[i + 1] - cuts[i]), from_n, 0, fold_dev) for i in range(pieces)
+        rows_of(rows - 1, span, from_n, 0, 5 if i == len(spans) - 1 else 0, fold_dev)
+        for i, span in enumerate(spans)
     ]
+    to_n = rows_of(rows - 1, every, from_s, 0, 1, n_dev)
+    to_s = rows_of(0, every, from_n, 1, 0, s_dev)
+    to_ss = [rows_of(0, span, from_n, 1, r, s_dev) for span, r in halves]
     to_e = send(ecol, west, 2, 2, e_dev)
     to_w = send(wcol, east, 3, 3, w_dev)
     to_relay = send(wcol, relay, 3, 4, (lon, lat_up))
     onward = send(relay, east, 4, 3, (n_lon - 1, lat_down))
 
     def tile(t, k):
-        return flat[pl.ds(t * plane + k * rows, rows), :]
+        return flat[pl.ds(lead * rows + t * plane + k * rows, rows), :]
 
     def density(k):
         return HALINE * tile(1, k) - THERMAL * tile(0, k)
-
-    starts = {0: 1}
-    while max(starts.values()) < pieces:
-        last = max(starts.values())
-        starts[last] = min(last + 2, pieces)
 
     def gather_columns(e_ref, w_ref, e_off, w_off, before=None):
         zeros = jnp.zeros((rows, lanes), jnp.float32)
@@ -182,15 +195,14 @@
             es[reg] = jnp.where(lane == (at + e_off) % lanes, value, es[reg])
             ws[reg] = jnp.where(lane == (at + w_off) % lanes, value, ws[reg])
 
-        for i in range(pieces):
-            if before is not None and i in starts:
-                for n in range(i, starts[i]):
-                    before(n)
+        for i in range(len(groups)):
+            if before is not None:
+                before(i)
             if i == 0:
                 place(kmt_own, per * slot, 0)
                 for k in range(levels):
                     place(density(k), k % per * slot + tracers, k // per)
-            for t in range(i * group, (i + 1) * group):
+            for t in range(ends[i], ends[i + 1]):
                 for k in range(levels):
                     place(tile(t, k), k % per * slot + t, k // per)
         for j in range(regs):
@@ -221,9 +233,8 @@
 
         @pl.when(inner)
         def _():
-            to_s.start()
-
-    held = max(pieces - 2, 1)
+            for copy in to_ss:
+                copy.start()
 
     def before(i):
         with jax.named_scope(f"load{i}"):
@@ -234,27 +245,23 @@
             def _():
                 enter()
 
-        if i < held:
+        if i < len(groups) - 1:
 
             @pl.when(late_top)
             def _():
                 folds[i].start()
 
-        if i == pieces - 1:
+        else:
 
             @pl.when(late_below)
             def _():
                 with jax.named_scope("barrier"):
                     enter()
 
-            @pl.when(late)
-            def _():
-                send_inner_rows()
-
     with jax.named_scope("loadk"):
         load_kmt.wait()
     kmt_own = kmt_int[...].astype(jnp.float32)
-    xv[tiles, :, :] = kmt_own
+    xv[lead - 1, :, :] = kmt_own
     gather_columns(ecol, wcol, 0, 1, before)
     with jax.named_scope("send"):
 
@@ -272,8 +279,11 @@
 
         @pl.when(late_top)
         def _():
-            for i in range(held, pieces):
-                folds[i].start()
+            folds[-1].start()
+
+        @pl.when(late)
+        def _():
+            send_inner_rows()
 
     with jax.named_scope("inner"):
         gather_columns(inner_e, inner_w, -1, 2)
@@ -330,7 +340,7 @@
         def _(i):
             fields = []
             for u in range(TOGETHER):
-                base = pl.multiple_of((i * TOGETHER + u) * plane, rows)
+                base = pl.multiple_of(lead * rows + (i * TOGETHER + u) * plane, rows)
                 field = []
                 for k in range(levels):
                     own = flat[pl.ds(base + k * rows, rows), :]
@@ -363,7 +373,8 @@
 
         @pl.when(at_top)
         def _():
-            fold.start()
+            for copy in folds:
+                copy.start()
 
     @pl.when(relays)
     def _():
@@ -380,7 +391,7 @@
         return jnp.where(level == levels - 1, 0.0, pltpu.roll(v, levels - 1, 0))
 
     def at_row(t, r):
-        return flat[pl.ds(t * plane + r, levels, stride=rows), :]
+        return flat[pl.ds(lead * rows + t * plane + r, levels, stride=rows), :]
 
     def row_column(t0, t1, kmt):
         wet = (jnp.broadcast_to(kmt, (levels, lanes)) > level_f).astype(jnp.float32)
@@ -389,12 +400,15 @@
     def own_row(r):
         return row_column(at_row(0, r), at_row(1, r), kmt_own[r : r + 1, :])
 
-    def fix_rows(source, r, r_in, north, turn):
+    def fix_rows(source, r, r_in, north, turn, parts):
         def halo(t):
-            h = source[pl.ds(t * levels, levels), :]
+            h = source[pl.ds(lead + t * levels, levels), :]
             return pick(h, lanes - 1 - lane) if turn else h
 
-        k = halo(tracers)[:1, :]
+        first, last, wait = parts[0]
+        wait()
+        k = jnp.broadcast_to(source[pl.ds(lead - 1, 1), :], (rows, lanes))
+        k = (pick(k, lanes - 1 - lane) if turn else k)[:1, :]
         out_c, in_c = row_column(halo(0), halo(1), k), own_row(r_in)
         p, m = (out_c, in_c) if north else (in_c, out_c)
         cc, cp, cm = line(own_row(r), p, m, up_s, dn_s)
@@ -403,25 +417,28 @@
         lo = [pltpu.roll(c[0], levels - 1, 0) for c in table]
         mid = [c[1] for c in table]
         hi = [pltpu.roll(c[2], 1, 0) for c in table]
-
-        batch = tracers // 2 if turn else group
-
-        @pl.loop(0, tracers // batch)
-        def _(i):
-            for u in range(batch):
-                t = i * batch + u
-                values = (at_row(t, r), halo(t), at_row(t, r_in))
-                above = total([c * v for c, v in zip(lo, values)])
-                same = total([c * v for c, v in zip(mid, values)])
-                below = total([c * v for c, v in zip(hi, values)])
-                place = pl.ds(t * plane + r, levels, stride=rows)
-                out_ref[place, :] = (
-                    out_ref[place, :] + same + pltpu.roll(above, 1, 0) + pltpu.roll(below, levels - 1, 0)
-                )
+        for n, (first, last, wait) in enumerate(parts):
+            if n:
+                wait()
+            count = last - first
+            batch = next(b for b in (16, 12, 8, 4, 2, 1) if count % b == 0 and (turn or b <= 8))
+
+            @pl.loop(0, count // batch)
+            def _(i, first=first, batch=batch):
+                for u in range(batch):
+                    t = first + i * batch + u
+                    values = (at_row(t, r), halo(t), at_row(t, r_in))
+                    above = total([c * v for c, v in zip(lo, values)])
+                    same = total([c * v for c, v in zip(mid, values)])
+                    below = total([c * v for c, v in zip(hi, values)])
+                    place = pl.ds(t * plane + r, levels, stride=rows)
+                    out_ref[place, :] = (
+                        out_ref[place, :] + same + pltpu.roll(above, 1, 0) + pltpu.roll(below, levels - 1, 0)
+                    )
 
     def fix_n(turn):
-        fold.wait_recv()
-        fix_rows(from_n, rows - 1, rows - 2, True, turn)
+        parts = [(0, ends[-2], to_ss[0].wait_recv), (ends[-2], tracers, to_ss[1].wait_recv)]
+        fix_rows(from_n, rows - 1, rows - 2, True, turn, parts)
 
     with jax.named_scope("fixs"):
 
@@ -429,7 +446,7 @@
         def _():
             to_n.wait_recv()
 
-        fix_rows(from_s, 0, 1, False, False)
+        fix_rows(from_s, 0, 1, False, False, [(0, tracers, lambda: None)])
 
     with jax.named_scope("fixn"):
 
@@ -493,27 +510,23 @@
 
 
 def finish(sizes, part_ref, add_ref, out_ref, stage, sem):
-    tracers, levels, rows, lanes, pieces = sizes
+    tracers, levels, rows, lanes = sizes
     plane = levels * rows
-    group = tracers // pieces
     lane = lax.broadcasted_iota(jnp.int32, (rows, lanes), 1)
-    ends = jnp.logical_or(lane == 0, lane == lanes - 1)
+    sides = jnp.logical_or(lane == 0, lane == lanes - 1)
     add = [add_ref[pl.ds(k * rows, rows), :] for k in range(levels)]
-    copies = []
-    for i in range(pieces):
-        with jax.named_scope(f"insert{i}"):
-            for t in range(i * group, (i + 1) * group):
-                for k in range(levels):
-                    term = pltpu.roll(add[k], (lanes - 2 * t) % lanes, 1)
-                    place = pl.ds(t * plane + k * rows, rows)
-                    stage[place, :] = part_ref[place, :] + jnp.where(ends, term, 0.0)
-            span = pl.ds(i * group * plane, group * plane)
-            copy = pltpu.make_async_copy(stage.at[span], out_ref.at[span], sem.at[i])
-            copy.start()
-            copies.append(copy)
+    with jax.named_scope("insert"):
+        for t in range(tracers):
+            for k in range(levels):
+                term = pltpu.roll(add[k], (lanes - 2 * t) % lanes, 1)
+                place = pl.ds(t * plane + k * rows, rows)
+                stage[place, :] = part_ref[place, :] + jnp.where(sides, term, 0.0)
+            if t % STORE == 0 or t == tracers - 1:
+                first = 0 if t == 0 else (t - 1) // STORE * STORE + 1
+                span = pl.ds(first * plane, (t + 1 - first) * plane)
+                pltpu.make_async_copy(stage.at[span], out_ref.at[span], sem).start()
     with jax.named_scope("written"):
-        for copy in copies:
-            copy.wait()
+        pltpu.make_async_copy(stage, out_ref, sem).wait()
 
 
 def solution(mesh):
@@ -524,38 +537,36 @@
         tiles = nt * levels
         per = (lanes - 2) // (nt + 2)
         regs = (levels + per - 1) // per
-        pieces = 5 if nt % 5 == 0 else 1
+        groups = (nt // 5, 2 * nt // 5, nt - nt // 5 - 2 * nt // 5)
         assert levels == rows and per > 0
 
         def vmem(*shape):
             return pltpu.VMEM(shape, jnp.float32)
 
         part, add = pl.pallas_call(
-            functools.partial(kernel, (nt, levels, rows, lanes, n_lon, n_lat, pieces)),
+            functools.partial(kernel, (nt, levels, rows, lanes, n_lon, n_lat, groups)),
             out_shape=[vmem(tiles * rows, lanes), vmem(levels * rows, lanes)],
             in_specs=[pl.BlockSpec(memory_space=pltpu.HBM), pl.BlockSpec(memory_space=pltpu.HBM)],
             out_specs=[pl.BlockSpec(memory_space=pltpu.VMEM)] * 2,
             scratch_shapes=[
-                vmem(tiles + 1, rows, lanes),
+                vmem(tiles + levels, rows, lanes),
                 pltpu.VMEM((rows, lanes), jnp.int32),
                 vmem(15 * levels * rows, lanes),
             ]
             + [vmem(regs * rows, lanes)] * 7
             + [vmem(tiles + rows, lanes)] * 2
             + [
-                pltpu.SemaphoreType.DMA((pieces + 1,)),
-                pltpu.SemaphoreType.DMA((5,)),
-                pltpu.SemaphoreType.DMA((5,)),
+                pltpu.SemaphoreType.DMA((6,)),
             ],
             compiler_params=pltpu.CompilerParams(collective_id=0, has_side_effects=True),
         )(tracers.reshape(tiles, rows, lanes), kmt)
         part, add = (pltpu.with_memory_space_constraint(v, pltpu.VMEM) for v in (part, add))
         out = pl.pallas_call(
-            functools.partial(finish, (nt, levels, rows, lanes, pieces)),
+            functools.partial(finish, (nt, levels, rows, lanes)),
             out_shape=jax.ShapeDtypeStruct((tiles * rows, lanes), jnp.float32),
             in_specs=[pl.BlockSpec(memory_space=pltpu.VMEM)] * 2,
             out_specs=pl.BlockSpec(memory_space=pltpu.HBM),
-            scratch_shapes=[vmem(tiles * rows, lanes), pltpu.SemaphoreType.DMA((pieces,))],
+            scratch_shapes=[vmem(tiles * rows, lanes), pltpu.SemaphoreType.DMA],
         )(part, add)
         return out.reshape(nt, levels, rows, lanes)
 

time: 11 us -> 10.8 us (0.982)
  Pallas kernels: 10.8 us -> 10.5 us
    pallas_call x1, Pallas kernels: 9.57 us -> 9.43 us  [local(): pl.pallas_call(functools.partial(kernel, (nt, levels, rows, lanes, n_lon,...]
where the time goes in v4:
time: 10.8 us; the launch traced here: 10.5 us
  Pallas kernels  10.5 us (97%)
    pallas_call x1, Pallas kernels, local(): pl.pallas_call(functools.partial(kernel, (nt, levels, rows, lanes, n_lon,...  9.43 us
    pallas_call x1, Pallas kernels, local(): pl.pallas_call(functools.partial(finish, (nt, levels, rows, lanes)), out_...  1.11 us

profile of v4, /device:TPU:0, one launch (start us, length us, event | category | flops | bytes accessed | tf_op | source)
XLA Modules:
  0.0 10.5 jit_solution(5322689901829582022)
XLA Ops:
  0.0 9.4 %shard_map.28 = (f32[2560,128]{1,0:T(8,128)S(1)}, f32[64,128]{1,0:T(8,128)S(1)}) custom-call(f32[320,8,128]{2,1,0:T(8,128)} %bitcast.2, s32[8,128]{1,0:T(8,128)} %kmt_ref.1), custom_call_target="tpu_custom_call" | custom-call | tf_op jit(solution)/shard_map/pallas_call | solution.py:546
  9.4 1.1 %shard_map.29 = f32[2560,128]{1,0:T(8,128)} custom-call(f32[2560,128]{1,0:T(8,128)S(1)} %get-tuple-element.7.part_ref, f32[64,128]{1,0:T(8,128)S(1)} %get-tuple-element.8.add_ref), custom_call_target="tpu_custom_call" | custom-call | tf_op jit(solution)/shard_map/pallas_call | solution.py:564

commit v5 on v4

--- a/solution.py
+++ b/solution.py
@@ -101,37 +101,11 @@
     plane = levels * rows
     lead = levels
     ends = [sum(groups[:i]) for i in range(len(groups) + 1)]
-    slot = tracers + 2
-    per = (lanes - 2) // slot
-    regs = (levels + per - 1) // per
-
-    barrier = pltpu.get_barrier_semaphore()
-
-    def greet(dev):
-        pl.semaphore_signal(barrier, inc=1, device_id=dev, device_id_type=MESH)
-
-    with jax.named_scope("greet"):
-        greet(w_dev)
-
-        @pl.when(near)
-        def _():
-            greet(e_dev)
-
-        @pl.when(far)
-        def _():
-            greet((0, lat_up))
-
-        @pl.when(at_top)
-        def _():
-            greet(fold_dev)
-
-        @pl.when(below_top)
-        def _():
-            greet(n_dev)
-
-        @pl.when(inner)
-        def _():
-            greet(s_dev)
+    split = ends[-2]
+    slots = (split + 2, tracers - split)
+    pers = tuple((lanes - 2) // slot for slot in slots)
+    shares = tuple((levels + per - 1) // per for per in pers)
+    kmt_at = pers[0] * slots[0]
 
     load_kmt = pltpu.make_async_copy(kmt_ref, kmt_int, load_sem.at[len(groups)])
     load_kmt.start()
@@ -146,6 +120,34 @@
             load(t * levels, levels, i).start()
     loads = [load(ends[i] * levels, groups[i] * levels, i) for i in range(len(groups))]
     flat = xv.reshape((lead + tiles) * rows, lanes)
+
+    barrier = pltpu.get_barrier_semaphore()
+
+    def greet(dev):
+        pl.semaphore_signal(barrier, inc=1, device_id=dev, device_id_type=MESH)
+
+    with jax.named_scope("greet"):
+        greet(w_dev)
+
+        @pl.when(near)
+        def _():
+            greet(e_dev)
+
+        @pl.when(far)
+        def _():
+            greet((0, lat_up))
+
+        @pl.when(at_top)
+        def _():
+            greet(fold_dev)
+
+        @pl.when(below_top)
+        def _():
+            greet(n_dev)
+
+        @pl.when(inner)
+        def _():
+            greet(s_dev)
 
     lane = lax.broadcasted_iota(jnp.int32, (rows, lanes), 1)
     row = lax.broadcasted_iota(jnp.int32, (rows, lanes), 0)
@@ -175,10 +177,14 @@
     to_n = rows_of(rows - 1, every, from_s, 0, 1, n_dev)
     to_s = rows_of(0, every, from_n, 1, 0, s_dev)
     to_ss = [rows_of(0, span, from_n, 1, r, s_dev) for span, r in halves]
-    to_e = send(ecol, west, 2, 2, e_dev)
-    to_w = send(wcol, east, 3, 3, w_dev)
+    cols = (pl.ds(0, shares[0] * rows), pl.ds(shares[0] * rows, shares[1] * rows))
+    far_dev = (n_lon - 1, lat_down)
+    to_e = [send(ecol.at[c], west.at[c], 2, (2, 6)[i], e_dev) for i, c in enumerate(cols)]
+    to_w = [send(wcol.at[c], east.at[c], 3, (3, 7)[i], w_dev) for i, c in enumerate(cols)]
+    onward = [send(relay.at[c], east.at[c], 4, (3, 7)[i], far_dev) for i, c in enumerate(cols)]
     to_relay = send(wcol, relay, 3, 4, (lon, lat_up))
-    onward = send(relay, east, 4, 3, (n_lon - 1, lat_down))
+    all_e, all_w = send(ecol, west, 2, 2, e_dev), send(wcol, east, 3, 3, w_dev)
+    all_onward = send(relay, east, 4, 3, far_dev)
 
     def tile(t, k):
         return flat[pl.ds(lead * rows + t * plane + k * rows, rows), :]
@@ -186,9 +192,13 @@
     def density(k):
         return HALINE * tile(1, k) - THERMAL * tile(0, k)
 
-    def gather_columns(e_ref, w_ref, e_off, w_off, before=None):
+    def where_is(t, k):
+        n, u = (0, t) if t < split else (1, t - split)
+        return k % pers[n] * slots[n] + u, n * shares[0] + k // pers[n]
+
+    def gather_columns(e_ref, w_ref, e_off, w_off, before=None, after=None):
         zeros = jnp.zeros((rows, lanes), jnp.float32)
-        es, ws = [zeros] * regs, [zeros] * regs
+        es, ws = [zeros] * sum(shares), [zeros] * sum(shares)
 
         def place(value, at, reg):
             value = pltpu.roll(value, at + 1, 1)
@@ -199,15 +209,20 @@
             if before is not None:
                 before(i)
             if i == 0:
-                place(kmt_own, per * slot, 0)
+                place(kmt_own, kmt_at, 0)
                 for k in range(levels):
-                    place(density(k), k % per * slot + tracers, k // per)
+                    at, reg = where_is(0, k)
+                    place(density(k), at + split, reg)
             for t in range(ends[i], ends[i + 1]):
                 for k in range(levels):
-                    place(tile(t, k), k % per * slot + t, k // per)
-        for j in range(regs):
-            e_ref[pl.ds(j * rows, rows), :] = es[j]
-            w_ref[pl.ds(j * rows, rows), :] = ws[j]
+                    place(tile(t, k), *where_is(t, k))
+            if ends[i + 1] in (split, tracers):
+                n = 0 if ends[i + 1] == split else 1
+                for j in range(n * shares[0], n * shares[0] + shares[n]):
+                    e_ref[pl.ds(j * rows, rows), :] = es[j]
+                    w_ref[pl.ds(j * rows, rows), :] = ws[j]
+                if after is not None:
+                    after(n)
 
     def enter():
         @pl.when(at_bottom)
@@ -251,27 +266,28 @@
             def _():
                 folds[i].start()
 
-        else:
+    def after(n):
+        if n == 0:
 
             @pl.when(late_below)
             def _():
                 with jax.named_scope("barrier"):
                     enter()
 
+        @pl.when(late)
+        def _():
+            to_e[n].start()
+
+        @pl.when(jnp.logical_and(late, direct))
+        def _():
+            to_w[n].start()
+
     with jax.named_scope("loadk"):
         load_kmt.wait()
     kmt_own = kmt_int[...].astype(jnp.float32)
     xv[lead - 1, :, :] = kmt_own
-    gather_columns(ecol, wcol, 0, 1, before)
+    gather_columns(ecol, wcol, 0, 1, before, after)
     with jax.named_scope("send"):
-
-        @pl.when(late)
-        def _():
-            to_e.start()
-
-        @pl.when(jnp.logical_and(late, direct))
-        def _():
-            to_w.start()
 
         @pl.when(relayed)
         def _():
@@ -367,8 +383,8 @@
     def _():
         with jax.named_scope("barrier"):
             enter()
-        to_e.start()
-        to_w.start()
+        for copy in to_e + to_w:
+            copy.start()
         send_inner_rows()
 
         @pl.when(at_top)
@@ -379,7 +395,8 @@
     @pl.when(relays)
     def _():
         to_relay.wait_recv()
-        onward.start()
+        for copy in onward:
+            copy.start()
 
     level = lax.broadcasted_iota(jnp.int32, (levels, lanes), 0)
     level_f = level.astype(jnp.float32)
@@ -456,37 +473,50 @@
 
     west_side = lane % 2 == 0
     spot = jnp.minimum((lane + 1) // 2 % (lanes // 2), tracers - 1)
-
-    def both(w_ref, e_ref, w_off, e_off, at, k):
-        base, span = k % per * slot, pl.ds(k // per * rows, rows)
-        w_at = (base + at + w_off + lanes) % lanes
-        e_at = (base + at + e_off + lanes) % lanes
-        return jnp.where(west_side, pick(w_ref[span, :], w_at), pick(e_ref[span, :], e_at))
-
-    def edge(w_ref, e_ref, w_off, e_off):
-        args = (w_ref, e_ref, w_off, e_off)
-        fixed = jnp.full((rows, lanes), tracers, jnp.int32)
-        values = jnp.stack([both(*args, spot, k) for k in range(levels)])
-        rho = jnp.stack([both(*args, fixed, k) for k in range(levels)])
-        kmt = both(*args, jnp.full((rows, lanes), per * slot, jnp.int32), 0)
+    low = spot < split
+    spots = (jnp.minimum(spot, split - 1), jnp.maximum(spot - split, 0))
+
+    def both(refs, offs, at, reg):
+        span = pl.ds(reg * rows, rows)
+        picked = [pick(ref[span, :], (at + off + lanes) % lanes) for ref, off in zip(refs, offs)]
+        return jnp.where(west_side, *picked)
+
+    def values_of(refs, offs, n):
+        return jnp.stack([both(refs, offs, k % pers[n] * slots[n] + spots[n], n * shares[0] + k // pers[n])
+                          for k in range(levels)])
+
+    def column_of(refs, offs):
+        fixed = jnp.zeros((rows, lanes), jnp.int32)
+        rho = jnp.stack([both(refs, offs, fixed + (where_is(0, k)[0] + split), where_is(0, k)[1])
+                         for k in range(levels)])
+        kmt = both(refs, offs, fixed + kmt_at, 0)
         wet = jnp.stack([(kmt > float(k)).astype(jnp.float32) for k in range(levels)])
-        return values, column(rho, wet, up3, dn3)
+        return column(rho, wet, up3, dn3)
+
+    def joined(first, second):
+        return jnp.stack([jnp.where(low, first[k], second[k]) for k in range(levels)])
+
+    def applied(c, v):
+        return c[1] * v + c[0] * up3(v) + c[2] * dn3(v)
 
     with jax.named_scope("fixc0"):
-        own, own_c = edge(wcol, ecol, 1, 0)
-        ins, ins_c = edge(inner_w, inner_e, 2, -1)
+        own_at, ins_at, outs_at = ((wcol, ecol), (1, 0)), ((inner_w, inner_e), (2, -1)), ((west, east), (0, 1))
+        own_c, ins_c = column_of(*own_at), column_of(*ins_at)
+        own, ins = (joined(values_of(*at, 0), values_of(*at, 1)) for at in (own_at, ins_at))
     with jax.named_scope("waitc"):
-        to_e.wait_recv()
-        to_w.wait_recv()
+        to_e[0].wait_recv()
+        to_w[0].wait_recv()
     with jax.named_scope("fixc1"):
-        outs, outs_c = edge(west, east, 0, 1)
-        table = line(own_c, outs_c, ins_c, up3, dn3)
-        values = (own, outs, ins)
-        above = total([c[0] * up3(v) for c, v in zip(table, values)])
-        same = total([c[1] * v for c, v in zip(table, values)])
-        below = total([c[2] * dn3(v) for c, v in zip(table, values)])
+        own_t, outs_t, ins_t = line(own_c, column_of(*outs_at), ins_c, up3, dn3)
+        some = applied(own_t, own) + applied(ins_t, ins)
+        outs_0 = values_of(*outs_at, 0)
+    with jax.named_scope("waitc2"):
+        to_e[1].wait_recv()
+        to_w[1].wait_recv()
+    with jax.named_scope("fixc2"):
+        add = some + applied(outs_t, joined(outs_0, values_of(*outs_at, 1)))
         for k in range(levels):
-            add_ref[pl.ds(k * rows, rows), :] = same[k] + above[k] + below[k]
+            add_ref[pl.ds(k * rows, rows), :] = add[k]
 
     with jax.named_scope("fixtop"):
 
@@ -501,12 +531,12 @@
         def _():
             to_s.wait_send()
 
-        to_e.wait_send()
-        to_w.wait_send()
+        all_e.wait_send()
+        all_w.wait_send()
 
         @pl.when(relays)
         def _():
-            onward.wait_send()
+            all_onward.wait_send()
 
 
 def finish(sizes, part_ref, add_ref, out_ref, stage, sem):
@@ -535,10 +565,11 @@
     def local(tracers, kmt):
         nt, levels, rows, lanes = tracers.shape
         tiles = nt * levels
-        per = (lanes - 2) // (nt + 2)
-        regs = (levels + per - 1) // per
-        groups = (nt // 5, 2 * nt // 5, nt - nt // 5 - 2 * nt // 5)
-        assert levels == rows and per > 0
+        cuts = (0, nt // 10, 3 * nt // 10, 6 * nt // 10, nt)
+        groups = tuple(b - a for a, b in zip(cuts, cuts[1:]))
+        slots = (cuts[-2] + 2, groups[-1])
+        regs = sum(-(-levels // ((lanes - 2) // slot)) for slot in slots)
+        assert levels == rows and groups[0] > 1
 
         def vmem(*shape):
             return pltpu.VMEM(shape, jnp.float32)
@@ -556,7 +587,7 @@
             + [vmem(regs * rows, lanes)] * 7
             + [vmem(tiles + rows, lanes)] * 2
             + [
-                pltpu.SemaphoreType.DMA((6,)),
+                pltpu.SemaphoreType.DMA((8,)),
             ],
             compiler_params=pltpu.CompilerParams(collective_id=0, has_side_effects=True),
         )(tracers.reshape(tiles, rows, lanes), kmt)

time: 10.8 us -> 10.6 us (0.981)
    pallas_call x1, Pallas kernels: 9.43 us -> 9.31 us  [local(): pl.pallas_call(functools.partial(kernel, (nt, levels, rows, lanes, n_lon,...]
where the time goes in v5:
time: 10.6 us; the launch traced here: 10.4 us
  Pallas kernels  10.4 us (98%)
    pallas_call x1, Pallas kernels, local(): pl.pallas_call(functools.partial(kernel, (nt, levels, rows, lanes, n_lon,...  9.31 us
    pallas_call x1, Pallas kernels, local(): pl.pallas_call(functools.partial(finish, (nt, levels, rows, lanes)), out_...  1.11 us

profile of v5, /device:TPU:0, one launch (start us, length us, event | category | flops | bytes accessed | tf_op | source)
XLA Modules:
  0.0 10.4 jit_solution(7010423369129464808)
XLA Ops:
  0.0 9.3 %shard_map.28 = (f32[2560,128]{1,0:T(8,128)S(1)}, f32[64,128]{1,0:T(8,128)S(1)}) custom-call(f32[320,8,128]{2,1,0:T(8,128)} %bitcast.2, s32[8,128]{1,0:T(8,128)} %kmt_ref.1), custom_call_target="tpu_custom_call" | custom-call | tf_op jit(solution)/shard_map/pallas_call | solution.py:577
  9.3 1.1 %shard_map.29 = f32[2560,128]{1,0:T(8,128)} custom-call(f32[2560,128]{1,0:T(8,128)S(1)} %get-tuple-element.7.part_ref, f32[64,128]{1,0:T(8,128)S(1)} %get-tuple-element.8.add_ref), custom_call_target="tpu_custom_call" | custom-call | tf_op jit(solution)/shard_map/pallas_call | solution.py:595
